TPU v7x, 32 devices: a whole 2x2x4 slice. The times are simulated.
32 devices in a mesh: band: 4 (over z), px: 4 (over x, core), py: 2 (over y).
Axes of the slice: x: 2, y: 2, z: 4, core: 2. Of those that a mesh axis runs over, the one named last changes fastest.
Arguments:
- orbitals: bfloat16 [4, 1024, 384], P('band', ('px', 'py')), may hold values from -0.01171875 to 0.01171875
- occupations: float32 [4], P('band'), may hold values from 0.2 to 2
- stick_map: int32 [2, 1024], P(None, 'px'), may hold values from 0 to 191, as said below
- core_density: float32 [192, 192, 192], P('py', 'px'), may hold values from 0.05 to 0.5
Outputs:
- potential: float32 [192, 192, 192], P('py', 'px')
- gradient: float32 [3, 192, 192, 192], P(None, 'py', 'px')
Inputs may be any that keep to these rules, and one draw needn't show every extreme that they name: `stick_map`: columns i * 128 * 2 to (i + 1) * 128 * 2 - 1 have x index from i * 48 to (i + 1) * 48 - 1; no two columns share a grid position.
All inputs are finite; a program needn't handle non-finite values.
Results may differ from a plain program's by a relative error of at most 0.0054.
Values may be sent and summed in bfloat16 or wider, within the bound.
No kernel may reach another device: no remote copies, remote signals or barrier semaphores. Data moves between devices by JAX's collectives and lax.ppermute only.
A program may use at most 128 MiB of HBM per device.

v0:
```python
import math
import jax
import jax.numpy as jnp
from jax import lax
from jax.sharding import PartitionSpec as P

SPACING = 0.25
PBE_KAPPA = 0.804
PBE_MU = 0.2195
SLATER_COEF = 0.75 * (3.0 / math.pi) ** (1.0 / 3.0)
REDUCED_SCALE = 4.0 * (3.0 * math.pi**2) ** (2.0 / 3.0)
HIGHEST_PREC = lax.Precision.HIGHEST


def complex_table(row_index, col_index, points, direction):
    product = row_index[:, None] * col_index[None, :] % points
    angles = 2.0 * math.pi / points * product.astype(jnp.float32)
    cosine = jnp.cos(angles)
    sine_part = direction * jnp.sin(angles)
    return jnp.stack([jnp.stack([cosine, sine_part], 1), jnp.stack([-sine_part, cosine], 1)], 0)


def freq_pair(positions, points):
    signed = jnp.where(positions <= points // 2, positions, positions - points).astype(jnp.float32)
    gradient_freq = jnp.where(positions == points // 2, 0.0, signed)
    return (signed, gradient_freq)


def swap_rows(values):
    return lax.all_to_all(values, "px", split_axis=1, concat_axis=0, tiled=True)


def swap_depth(values):
    moved = lax.all_to_all(values, ("band", "py"), split_axis=1, concat_axis=0, tiled=True)
    return moved


def exchange_part(density, fields):
    cube_root = jnp.cbrt(density)
    four_thirds = density * cube_root
    grad_square = fields[1] * fields[1] + fields[2] * fields[2] + fields[3] * fields[3]
    reduced = grad_square / (REDUCED_SCALE * four_thirds * four_thirds)
    denominator = 1.0 + PBE_MU * reduced / PBE_KAPPA
    enhance = 1.0 + PBE_KAPPA - PBE_KAPPA / denominator
    enhance_slope = PBE_MU / (denominator * denominator)
    potential = fields[0] - SLATER_COEF * cube_root * (
        4.0 / 3.0 * enhance - 8.0 / 3.0 * reduced * enhance_slope
    )
    return jnp.concatenate([potential[None], fields[1:]], 0)


def transform(rho_local, pieces, depth_index, px_index):
    zshare, y_rows, points = rho_local.shape
    rows_px = lax.axis_size("px")
    rows_py = lax.axis_size("py")
    xblock = points // rows_px
    kyblock = points // pieces
    zblock = zshare * (pieces // rows_py)
    every_index = jnp.arange(points, dtype=jnp.int32)
    forward = complex_table(every_index, every_index, points, -1.0)
    x_table = forward[0].reshape(points, 2, rows_px, xblock).transpose(0, 2, 1, 3)
    section_data = jnp.einsum("zyx,xbsk->ybzsk", rho_local, x_table, precision=HIGHEST_PREC)
    section_data = swap_rows(section_data.reshape(y_rows, rows_px, zshare * 2 * xblock))
    section_data = section_data.reshape(points, zshare, 2, xblock)
    y_table = forward.reshape(2, points, 2, pieces, kyblock)
    section_data = jnp.einsum("yzrx,rysdk->zdksx", section_data, y_table, precision=HIGHEST_PREC)
    section_data = swap_depth(section_data.reshape(zshare, pieces, kyblock * 2 * xblock))
    section_data = section_data.reshape(pieces * zshare, kyblock, 2, xblock)
    source = jnp.arange(pieces * zshare, dtype=jnp.int32)
    device = source // zshare
    within = source % zshare
    z_order = device % rows_py * zblock + device // rows_py * zshare + within
    z_table = complex_table(z_order, every_index, points, -1.0)
    spectrum = jnp.einsum("zyrx,rzsk->kysx", section_data, z_table, precision=HIGHEST_PREC)
    q_depth, g_depth = freq_pair(every_index, points)
    ky_index = depth_index * kyblock + jnp.arange(kyblock, dtype=jnp.int32)
    q_col, g_col = freq_pair(ky_index, points)
    kx_index = px_index * xblock + jnp.arange(xblock, dtype=jnp.int32)
    q_row, g_row = freq_pair(kx_index, points)
    wave_unit = 2.0 * math.pi / (points * SPACING)
    squared = wave_unit**2 * (
        q_depth[:, None, None] ** 2 + q_col[None, :, None] ** 2 + q_row[None, None, :] ** 2
    )
    hartree = jnp.where(squared > 0, 4.0 * math.pi / jnp.where(squared > 0, squared, 1.0), 0.0)
    wave_z = wave_unit * g_depth[:, None, None]
    wave_y = wave_unit * g_col[None, :, None]
    wave_x = wave_unit * g_row[None, None, :]
    real_part = spectrum[:, :, 0, :]
    imag_part = spectrum[:, :, 1, :]
    first_factor = hartree - wave_x
    packed = jnp.stack(
        [
            jnp.stack([first_factor * real_part, first_factor * imag_part], 2),
            jnp.stack(
                [-wave_z * real_part - wave_y * imag_part, wave_y * real_part - wave_z * imag_part],
                2,
            ),
        ],
        0,
    )
    inverse = complex_table(every_index, every_index, points, 1.0)
    zi_table = complex_table(every_index, z_order, points, 1.0).reshape(
        2, points, 2, pieces, zshare
    )
    section_data = jnp.einsum("fkyrx,rksdz->ydfzsx", packed, zi_table, precision=HIGHEST_PREC)
    section_data = swap_depth(section_data.reshape(kyblock, pieces, 2 * zshare * 2 * xblock))
    section_data = section_data.reshape(points, 2, zshare, 2, xblock)
    yi_table = inverse.reshape(2, points, 2, rows_px, y_rows)
    section_data = jnp.einsum("kfzrx,rksby->xbfzsy", section_data, yi_table, precision=HIGHEST_PREC)
    section_data = swap_rows(section_data.reshape(xblock, rows_px, 2 * zshare * 2 * y_rows))
    section_data = section_data.reshape(points, 2, zshare, 2, y_rows)
    fields = jnp.einsum("kfzry,rksx->fszyx", section_data, inverse, precision=HIGHEST_PREC)
    fields = fields * (1.0 / float(points) ** 3)
    return fields.reshape(4, zshare, y_rows, points)


def body(orbitals, occupations, stick_map, core_density):
    bands_here, columns_here, doubled = orbitals.shape
    points = doubled // 2
    rows_px = lax.axis_size("px")
    rows_py = lax.axis_size("py")
    groups = lax.axis_size("band")
    px_index = lax.axis_index("px")
    py_index = lax.axis_index("py")
    xblock = points // rows_px
    zblock = points // rows_py
    y_rows = points // rows_px
    every_index = jnp.arange(points, dtype=jnp.int32)
    inverse = complex_table(every_index, every_index, points, 1.0)
    z_table = (
        inverse.reshape(2, points, 2, rows_py, zblock)
        .transpose(0, 1, 3, 2, 4)
        .reshape(doubled, doubled)
    )
    columns = jnp.dot(
        orbitals.astype(jnp.float32).reshape(bands_here * columns_here, doubled),
        z_table,
        precision=HIGHEST_PREC,
    )
    columns = columns.astype(jnp.bfloat16).reshape(bands_here, columns_here, doubled)
    columns = lax.all_to_all(columns, "py", split_axis=2, concat_axis=1, tiled=True)
    slot_index = stick_map[1] * xblock + (stick_map[0] - px_index * xblock)
    plane_data = (
        jnp.zeros((bands_here, points * xblock, 2 * zblock), jnp.float32)
        .at[:, slot_index]
        .set(columns.astype(jnp.float32))
    )
    plane_data = plane_data.reshape(bands_here, points, xblock, 2, zblock)
    plane_data = jnp.einsum("byxrz,rysk->bkxsz", plane_data, inverse, precision=HIGHEST_PREC)
    plane_data = plane_data.astype(jnp.bfloat16).reshape(bands_here, points, xblock * 2 * zblock)
    plane_data = lax.all_to_all(plane_data, "px", split_axis=1, concat_axis=2, tiled=True)
    plane_data = plane_data.astype(jnp.float32).reshape(bands_here, y_rows, points, 2, zblock)
    orbital_values = jnp.einsum("byxrz,rxsk->bszyk", plane_data, inverse, precision=HIGHEST_PREC)
    density = jnp.einsum(
        "b,bszyk->zyk", occupations, orbital_values * orbital_values, precision=HIGHEST_PREC
    )
    zshare = zblock // groups
    band_index = lax.axis_index("band")
    shared_rows = lax.psum_scatter(density, "band", scatter_dimension=0, tiled=True)
    core_rows = lax.dynamic_slice_in_dim(core_density, band_index * zshare, zshare, 0)
    rho_local = shared_rows + core_rows
    fields = transform(rho_local, groups * rows_py, band_index * rows_py + py_index, px_index)
    results = lax.all_gather(exchange_part(rho_local, fields), "band", axis=1, tiled=True)
    return (results[0], results[1:4])


def solution(mesh):
    return jax.shard_map(
        body,
        mesh=mesh,
        in_specs=(P("band", ("px", "py"), None), P("band"), P(None, "px"), P("py", "px", None)),
        out_specs=(P("py", "px", None), P(None, "py", "px", None)),
        check_vma=False,
    )
```

profile of v0, /device:TPU:0, one launch (start us, length us, event | category | flops | bytes accessed | tf_op | source)
XLA Modules:
  0.0 1160.9 jit_solution(13728535052132577211)
XLA Ops:
  7.2 0.8 fusion.90
  10.8 1.2 reduce.3
  12.6 4.3 all-to-all-start
  16.9 0.8 fusion.121
  17.7 0.8 fusion.111
  18.6 2.7 all-to-all-done
  21.9 5.9 scatter_custom_fusion
  27.8 12.3 %reshape.807 = f32[192,48,2,96]{3,2,1,0:T(2,128)} reshape(f32[9216,192]{1,0:T(8,128)} %scatter_custom_fusion) | data formatting | bytes 14155776 | tf_op jit(solution)/shard_map/reshape.2
  40.1 14.2 %copy.140 = f32[192,48,2,96]{0,3,2,1:T(8,128)} copy(f32[192,48,2,96]{3,2,1,0:T(2,128)} %reshape.807) | data formatting | bytes 14155776 | tf_op jit(solution)/shard_map/reshape.2
  54.3 18.6 %fusion.5 = bf16[1,192,48,2,96]{1,4,2,3,0:T(8,128)(2,1)} fusion(f32[192,48,2,96]{0,3,2,1:T(8,128)} %copy.140, f32[1,192,2,192]{3,1,0,2:T(8,128)S(1)} %get-tuple-element.11, f32[1,192,2,192]{3,1,0,2:T(8,128)S(1)} %get-tuple-element.10), kind=kOutput, calls=%fused_computation.8 | convolution fusion | flops 8155643904 | bytes 11206656 | tf_op jit(solution)/shard_map/byxrz,rysk->bkxsz/dot_general | solution.py:149
  72.8 11.6 copy.141
  84.4 24.4 %reshape.857 = bf16[1,192,9216]{2,0,1:T(2,128)(2,1)} reshape(bf16[1,192,48,2,96]{4,3,2,1,0:T(2,128)(2,1)} %copy.141) | data formatting | bytes 7077888 | tf_op jit(solution)/shard_map/reshape | solution.py:150
  108.8 78.5 %reduce.4 = bf16[192,9216]{1,0:T(8,128)(2,1)} reduce(bf16[192,1,9216]{2,1,0:T(2,128)(2,1)} %bitcast.221, bf16[]{:T(256)} %broadcast.1309), dimensions={1}, to_apply=%bitcast.207.reduce_sub_computation | reduce | bytes 7077890
  187.3 5.6 reshape.864
  192.9 4.7 all-to-all-start.1
  198.3 40.5 %all-to-all-done.1 = bf16[4,2,221184]{2,1,0:T(2,128)(2,1)} async-done(((bf16[4,2,221184]{2,1,0:T(2,128)(2,1)}), bf16[4,2,221184]{2,1,0:T(2,128)(2,1)}, u32[]{:S(2)}, u32[]{:S(2)}) %all-to-all-start.1) | async-done | bytes 3538976 | tf_op jit(solution)/shard_map/all_to_all | solution.py:151
  238.8 6.6 reshape.865
  245.4 4.1 copy.194
  249.5 4.5 copy.143
  254.0 14.9 %reshape.809 = bf16[48,192,2,96]{3,2,1,0:T(2,128)(2,1)} reshape(bf16[1,48,4,9216]{3,2,1,0:T(4,128)(2,1)} %copy.143) | data formatting | bytes 7077888 | tf_op jit(solution)/shard_map/reshape.5
  268.9 10.5 fusion.2
  279.5 2.5 multiply_bitcast_fusion
  282.0 6.8 copy.146
  288.8 0.9 fusion.94
  289.7 84.4 %reduce-scatter.2.cloned.1.call-done = f32[24,48,192]{2,1,0:T(8,128)} async-done(((f32[96,48,192]{2,1,0:T(8,128)}), f32[24,48,192]{2,1,0:T(8,128)}) %reduce-scatter.2.cloned.1.call-update) | async-done | bytes 884752 | tf_op jit(solution)/shard_map/reduce_scatter | solution.py:159
  374.1 6.7 convolution_bitcast_fusion
  380.9 7.5 copy.147
  388.4 9.3 reshape.811
  397.7 3.8 all-to-all-start.2
  401.5 0.9 sine_multiply_fusion.1
  402.4 21.2 %all-to-all-done.2 = f32[48,4,2304]{2,0,1:T(8,128)S(1)} async-done(((f32[48,4,2304]{2,0,1:T(8,128)}), f32[48,4,2304]{2,0,1:T(8,128)S(1)}, u32[]{:S(2)}, u32[]{:S(2)}) %all-to-all-start.2) | async-done | bytes 1769504 | tf_op jit(solution)/shard_map/all_to_all | solution.py:30
  423.6 8.6 reshape.812
  432.2 10.4 fusion.27
  442.6 5.8 copy.186
  448.4 9.7 reshape.858
  458.1 5.1 all-to-all-start.3
  463.3 0.9 sine_multiply_fusion.2
  464.2 0.9 maximum_bitcast_fusion.14
  465.2 1.6 fusion.103
  466.9 37.3 %all-to-all-done.3 = f32[24,8,2304]{2,0,1:T(8,128)S(1)} async-done(((f32[24,8,2304]{2,0,1:T(8,128)}), f32[24,8,2304]{2,0,1:T(8,128)S(1)}, u32[]{:S(2)}, u32[]{:S(2)}) %all-to-all-start.3) | async-done | bytes 1769504 | tf_op jit(solution)/shard_map/all_to_all | solution.py:34
  504.1 8.6 reshape.814
  512.7 5.7 copy.152
  518.4 5.1 fusion.34
  523.6 0.8 slice_multiply_fusion.4
  525.6 15.9 %fusion.22 = f32[24,8,2,24,2,48]{5,3,0,2,1,4:T(8,128)S(1)} fusion(f32[1,192,24,2,48]{1,4,2,3,0:T(8,128)S(1)} %maximum_bitcast_fusion.5, f32[1,192,24,2,48]{1,4,2,3,0:T(8,128)S(1)} %maximum_bitcast_fusion.4, f32[1,192,1,8,24]{1,4,0,3,2:T(8,128)S(1)} %copy-done.4, f32[1,192,1,8,24]{1,4,0,3,2:T(8,128)S(1)} %copy-done.3, ...), kind=kOutput, calls=%fused_computation.28 | convolution fusion | flops 4078190592 | bytes 7520256 | tf_op jit(solution)/shard_map/fkyrx,rksdz->ydfzsx/dot_general | solution.py:105
  541.5 8.0 copy.189
  549.5 16.6 %reshape.859 = f32[24,8,4608]{2,0,1:T(8,128)} reshape(f32[24,8,2,24,2,48]{5,4,3,2,0,1:T(2,128)} %copy.189) | data formatting | bytes 7077888 | tf_op jit(solution)/shard_map/reshape | solution.py:106
  566.1 4.5 all-to-all-start.4
  570.6 0.9 fusion.107
  571.5 77.6 %all-to-all-done.4 = f32[24,8,4608]{2,0,1:T(8,128)} async-done(((f32[24,8,4608]{2,0,1:T(8,128)}), f32[24,8,4608]{2,0,1:T(8,128)}, u32[]{:S(2)}, u32[]{:S(2)}) %all-to-all-start.4) | async-done | bytes 3538976 | tf_op jit(solution)/shard_map/all_to_all | solution.py:34
  649.2 17.3 %reshape.816 = f32[192,2,24,2,48]{4,3,2,1,0:T(2,128)} reshape(f32[8,24,1,4608]{3,1,0,2:T(8,128)} %bitcast.63) | data formatting | bytes 7077888 | tf_op jit(solution)/shard_map/reshape | solution.py:107
  666.5 24.9 %fusion.19 = f32[48,4,2,24,2,48]{0,5,3,2,1,4:T(8,128)} fusion(f32[192,2,24,2,48,1,1]{4,3,2,1,0,6,5:T(2,128)} %bitcast.218, f32[1,192,1,4,48]{1,4,0,3,2:T(8,128)S(1)} %get-tuple-element.20, f32[1,192,1,4,48]{1,4,0,3,2:T(8,128)S(1)} %get-tuple-element.19, f32[1,192,1,4,48]{1,4,0,3,2:T(8,128)S(1)} %get-tuple-element.18), kind=kOutput, calls=%fused_computation.27 | convolution fusion | flops 4077305856 | bytes 7520256 | tf_op jit(solution)/shard_map/kfzrx,rksby->xbfzsy/dot_general | solution.py:109
  691.4 13.7 %copy.157 = f32[48,4,2,24,2,48]{5,4,3,2,0,1:T(2,128)} copy(f32[48,4,2,24,2,48]{0,5,3,2,1,4:T(8,128)} %fusion.19) | data formatting | bytes 7077888 | tf_op jit(solution)/shard_map/kfzrx,rksby->xbfzsy/transpose | solution.py:109
  705.1 16.6 %reshape.817 = f32[48,4,4608]{2,0,1:T(8,128)} reshape(f32[48,4,2,24,2,48]{5,4,3,2,0,1:T(2,128)} %copy.157) | data formatting | bytes 7077888 | tf_op jit(solution)/shard_map/reshape | solution.py:110
  721.7 46.9 %all_to_all.84 = f32[48,4,4608]{2,0,1:T(8,128)} all-to-all(f32[48,4,4608]{2,0,1:T(8,128)} %reshape.817), channel_id=1, replica_groups=mesh['band'=4,'px'=4,'py'=2] {'px'}, dimensions={1} | all-to-all | bytes 7077888 | tf_op jit(solution)/shard_map/all_to_all | solution.py:30
  768.6 17.1 %reshape.818 = f32[192,2,24,2,48]{4,3,2,1,0:T(2,128)} reshape(f32[4,48,1,4608]{3,1,0,2:T(8,128)} %bitcast.224) | data formatting | bytes 7077888 | tf_op jit(solution)/shard_map/reshape | solution.py:111
  785.7 13.2 %copy.158 = f32[192,2,24,2,48]{0,4,3,2,1:T(8,128)} copy(f32[192,2,24,2,48]{4,3,2,1,0:T(2,128)} %reshape.818) | data formatting | bytes 7077888 | tf_op jit(solution)/shard_map/reshape | solution.py:111
  798.9 10.3 fusion.9
  809.8 1.0 copy-done.2
  810.8 3.1 fusion.41
  814.0 2.6 pad_maximum_fusion
  816.6 320.4 %all-gather.2.cloned.1.call-done = f32[4,96,48,192]{3,2,1,0:T(8,128)} async-done(((f32[4,24,48,192]{3,2,1,0:T(8,128)}), f32[4,96,48,192]{3,2,1,0:T(8,128)}) %all-gather.2.cloned.1.call-update) | async-done | bytes 14155792 | tf_op jit(solution)/shard_map/all_gather | solution.py:163
  1137.0 4.8 slice_bitcast_fusion
  1141.8 11.8 %slice.55 = f32[3,96,48,192]{3,2,1,0:T(8,128)} slice(f32[4,96,48,192]{3,2,1,0:T(8,128)} %all-gather.2.cloned.1.call-done), slice={[1:4], [0:96], [0:48], [0:192]} | slice | bytes 21233664 | tf_op jit(solution)/shard_map/slice | solution.py:164
  (42 shorter events, 6.1 us)
Async XLA Ops:
  7.2 2.2 copy-start
  8.1 10.4 copy-start.5
  12.6 8.6 all-to-all-start
  192.9 45.9 %all-to-all-start.1 = ((bf16[4,2,221184]{2,1,0:T(2,128)(2,1)}), bf16[4,2,221184]{2,1,0:T(2,128)(2,1)}, u32[]{:S(2)}, u32[]{:S(2)}) async-start(bf16[4,2,221184]{2,1,0:T(2,128)(2,1)} %reshape.864), calls=%async_computation.1 | async-start | bytes 7077888 | tf_op jit(solution)/shard_map/all_to_all | solution.py:151
  197.6 176.5 %reduce-scatter.2.cloned.1.call-start = ((), (), s32[]{:S(2)}) async-start(), calls=%async_computation.7 | async-start | bytes 5898240 | tf_op jit(solution)/shard_map/reduce_scatter | solution.py:159
  397.7 25.9 %all-to-all-start.2 = ((f32[48,4,2304]{2,0,1:T(8,128)}), f32[48,4,2304]{2,0,1:T(8,128)S(1)}, u32[]{:S(2)}, u32[]{:S(2)}) async-start(f32[48,4,2304]{2,0,1:T(8,128)} %reshape.811), calls=%async_computation.3 | async-start | bytes 3538944 | tf_op jit(solution)/shard_map/all_to_all | solution.py:30
  458.1 46.0 %all-to-all-start.3 = ((f32[24,8,2304]{2,0,1:T(8,128)}), f32[24,8,2304]{2,0,1:T(8,128)S(1)}, u32[]{:S(2)}, u32[]{:S(2)}) async-start(f32[24,8,2304]{2,0,1:T(8,128)} %reshape.858), calls=%async_computation.4 | async-start | bytes 3538944 | tf_op jit(solution)/shard_map/all_to_all | solution.py:34
  524.6 0.9 copy-start.3
  524.6 1.0 copy-start.4
  566.1 83.1 %all-to-all-start.4 = ((f32[24,8,4608]{2,0,1:T(8,128)}), f32[24,8,4608]{2,0,1:T(8,128)}, u32[]{:S(2)}, u32[]{:S(2)}) async-start(f32[24,8,4608]{2,0,1:T(8,128)} %reshape.859), calls=%async_computation.5 | async-start | bytes 7077888 | tf_op jit(solution)/shard_map/all_to_all | solution.py:34
  570.6 566.4 %all-gather.2.cloned.1.call-start = ((), (), s32[]{:S(2)}) async-start(), calls=%async_computation.8 | async-start | bytes 23592960 | tf_op jit(solution)/shard_map/all_gather | solution.py:163
  809.6 1.3 copy-start.2
  1141.8 11.8 %copy-start.1 = (bf16[1,128,384]{2,1,0:T(8,128)(2,1)S(1)}, bf16[1,128,384]{2,1,0:T(8,128)(2,1)}, u32[]{:S(2)}) copy-start(bf16[1,128,384]{2,1,0:T(8,128)(2,1)} %param.4) | copy-start | bytes 294916
Sparse Core Ops, SparseCore 0:
  288.9 85.1 reduce-scatter.1
  816.7 320.2 all-gather.1
where the time goes:
time: 1170 us; the launch traced here: 1160 us
  waiting for transfers between devices  584 us (50%)
  local copies, waits for them, and re-layouts  291 us (25%)
  matrix products  103 us (9%)
  other arithmetic  98.1 us (8%)
  blocking collectives  46.9 us (4%)
  starting transfers between devices  22.4 us (2%)
  between operations  15.5 us (1%)
    all_gather x1, waiting for transfers between devices, body(): lax.all_gather(exchange_part(rho_local, fields), 'band', axis=1, tiled=True)  320 us
    all_to_all x2, waiting for transfers between devices, swap_depth(): lax.all_to_all(values, ('band', 'py'), split_axis=1, concat_axis=0, tiled...  115 us
    reduce_scatter x1, waiting for transfers between devices, body(): lax.psum_scatter(density, 'band', scatter_dimension=0, tiled=True)  84.4 us
    unnamed x2, other arithmetic  79.7 us
    all_to_all x1, blocking collectives, swap_rows(): return lax.all_to_all(values, 'px', split_axis=1, concat_axis=0, tiled=True)  46.9 us
    another operation x3, local copies, waits for them, and re-layouts  41.4 us
    all_to_all x1, waiting for transfers between devices, body(): lax.all_to_all(plane_data, 'px', split_axis=1, concat_axis=2, tiled=True)  40.5 us
    reshape x2, local copies, waits for them, and re-layouts, transform(): section_data = section_data.reshape(points, 2, zshare, 2, y_rows)  30.3 us
  transfers between devices with their start and end apart: 7, of which 7 were waited for; matrix products, arithmetic and copies ran while one was open for 1% of the time, Pallas kernels for 0%

commit v1 on v0

--- a/solution.py
+++ b/solution.py
@@ -115,6 +115,11 @@
 
 
 def body(orbitals, occupations, stick_map, core_density):
+
+    def _read_sections(message, lane_axis):
+        answer = lax.all_gather(message, lane_axis)
+        return jnp.concatenate(answer, axis=1)
+
     bands_here, columns_here, doubled = orbitals.shape
     points = doubled // 2
     rows_px = lax.axis_size("px")
@@ -160,7 +165,7 @@
     core_rows = lax.dynamic_slice_in_dim(core_density, band_index * zshare, zshare, 0)
     rho_local = shared_rows + core_rows
     fields = transform(rho_local, groups * rows_py, band_index * rows_py + py_index, px_index)
-    results = lax.all_gather(exchange_part(rho_local, fields), "band", axis=1, tiled=True)
+    results = _read_sections(exchange_part(rho_local, fields), "band")
     return (results[0], results[1:4])
 
 

time: 1170 us -> 1180 us (level)
    slice x1 -> x3, local copies, waits for them, and re-layouts: 11.8 us -> 28.1 us  [body(): return (results[0], results[1:4])]
where the time goes in v1:
time: 1180 us; the launch traced here: 1170 us
  waiting for transfers between devices  585 us (50%)
  local copies, waits for them, and re-layouts  302 us (26%)
  matrix products  103 us (9%)
  other arithmetic  98.1 us (8%)
  blocking collectives  46.9 us (4%)
  starting transfers between devices  22.4 us (2%)
  between operations  15.5 us (1%)
    all_gather x1, waiting for transfers between devices, _read_sections(): answer = lax.all_gather(message, lane_axis)  321 us
    all_to_all x2, waiting for transfers between devices, swap_depth(): lax.all_to_all(values, ('band', 'py'), split_axis=1, concat_axis=0, tiled...  115 us
    reduce_scatter x1, waiting for transfers between devices, body(): lax.psum_scatter(density, 'band', scatter_dimension=0, tiled=True)  84.4 us
    unnamed x2, other arithmetic  79.7 us
    all_to_all x1, blocking collectives, swap_rows(): return lax.all_to_all(values, 'px', split_axis=1, concat_axis=0, tiled=True)  46.9 us
    another operation x3, local copies, waits for them, and re-layouts  41.4 us
    all_to_all x1, waiting for transfers between devices, body(): lax.all_to_all(plane_data, 'px', split_axis=1, concat_axis=2, tiled=True)  40.5 us
    reshape x2, local copies, waits for them, and re-layouts, transform(): section_data = section_data.reshape(points, 2, zshare, 2, y_rows)  30.3 us
  transfers between devices with their start and end apart: 7, of which 7 were waited for; matrix products, arithmetic and copies ran while one was open for 1% of the time, Pallas kernels for 0%

profile of v1, /device:TPU:0, one launch (start us, length us, event | category | flops | bytes accessed | tf_op | source)
XLA Modules:
  0.0 1173.2 jit_solution(14635793057027786476)
XLA Ops:
  7.2 0.8 fusion.90
  10.8 1.2 reduce.3
  12.6 4.3 all-to-all-start
  17.7 0.8 fusion.111
  18.6 2.7 all-to-all-done
  21.9 5.9 scatter_custom_fusion
  27.8 12.3 %reshape.814 = f32[192,48,2,96]{3,2,1,0:T(2,128)} reshape(f32[9216,192]{1,0:T(8,128)} %scatter_custom_fusion) | data formatting | bytes 14155776 | tf_op jit(solution)/shard_map/reshape.2
  40.1 14.2 %copy.146 = f32[192,48,2,96]{0,3,2,1:T(8,128)} copy(f32[192,48,2,96]{3,2,1,0:T(2,128)} %reshape.814) | data formatting | bytes 14155776 | tf_op jit(solution)/shard_map/reshape.2
  54.3 18.6 %fusion.5 = bf16[1,192,48,2,96]{1,4,2,3,0:T(8,128)(2,1)} fusion(f32[192,48,2,96]{0,3,2,1:T(8,128)} %copy.146, f32[1,192,2,192]{3,1,0,2:T(8,128)S(1)} %get-tuple-element.11, f32[1,192,2,192]{3,1,0,2:T(8,128)S(1)} %get-tuple-element.10), kind=kOutput, calls=%fused_computation.8 | convolution fusion | flops 8155643904 | bytes 11206656 | tf_op jit(solution)/shard_map/byxrz,rysk->bkxsz/dot_general | solution.py:154
  72.8 11.6 copy.147
  84.4 24.4 %reshape.866 = bf16[1,192,9216]{2,0,1:T(2,128)(2,1)} reshape(bf16[1,192,48,2,96]{4,3,2,1,0:T(2,128)(2,1)} %copy.147) | data formatting | bytes 7077888 | tf_op jit(solution)/shard_map/reshape | solution.py:155
  108.8 78.5 %reduce.4 = bf16[192,9216]{1,0:T(8,128)(2,1)} reduce(bf16[192,1,9216]{2,1,0:T(2,128)(2,1)} %bitcast.224, bf16[]{:T(256)} %broadcast.1309), dimensions={1}, to_apply=%bitcast.210.reduce_sub_computation | reduce | bytes 7077890
  187.3 5.6 reshape.873
  192.9 4.7 all-to-all-start.1
  198.3 40.5 %all-to-all-done.1 = bf16[4,2,221184]{2,1,0:T(2,128)(2,1)} async-done(((bf16[4,2,221184]{2,1,0:T(2,128)(2,1)}), bf16[4,2,221184]{2,1,0:T(2,128)(2,1)}, u32[]{:S(2)}, u32[]{:S(2)}) %all-to-all-start.1) | async-done | bytes 3538976 | tf_op jit(solution)/shard_map/all_to_all | solution.py:156
  238.8 6.6 reshape.874
  245.4 4.1 copy.201
  249.5 4.5 copy.149
  254.0 14.9 %reshape.816 = bf16[48,192,2,96]{3,2,1,0:T(2,128)(2,1)} reshape(bf16[1,48,4,9216]{3,2,1,0:T(4,128)(2,1)} %copy.149) | data formatting | bytes 7077888 | tf_op jit(solution)/shard_map/reshape.5
  268.9 10.5 fusion.2
  279.5 2.5 multiply_bitcast_fusion
  282.0 6.8 copy.152
  288.8 0.9 fusion.94
  289.7 84.4 %reduce-scatter.2.cloned.1.call-done = f32[24,48,192]{2,1,0:T(8,128)} async-done(((f32[96,48,192]{2,1,0:T(8,128)}), f32[24,48,192]{2,1,0:T(8,128)}) %reduce-scatter.2.cloned.1.call-update) | async-done | bytes 884752 | tf_op jit(solution)/shard_map/reduce_scatter | solution.py:164
  374.1 6.7 convolution_bitcast_fusion
  380.9 7.5 copy.153
  388.4 9.3 reshape.818
  397.7 3.8 all-to-all-start.2
  401.5 0.9 sine_multiply_fusion.1
  402.4 21.2 %all-to-all-done.2 = f32[48,4,2304]{2,0,1:T(8,128)S(1)} async-done(((f32[48,4,2304]{2,0,1:T(8,128)}), f32[48,4,2304]{2,0,1:T(8,128)S(1)}, u32[]{:S(2)}, u32[]{:S(2)}) %all-to-all-start.2) | async-done | bytes 1769504 | tf_op jit(solution)/shard_map/all_to_all | solution.py:30
  423.6 8.6 reshape.819
  432.2 10.4 fusion.27
  442.6 5.8 copy.193
  448.4 9.7 reshape.867
  458.1 5.1 all-to-all-start.3
  463.3 0.9 sine_multiply_fusion.2
  464.2 0.9 maximum_bitcast_fusion.14
  465.2 1.6 fusion.103
  466.9 37.3 %all-to-all-done.3 = f32[24,8,2304]{2,0,1:T(8,128)S(1)} async-done(((f32[24,8,2304]{2,0,1:T(8,128)}), f32[24,8,2304]{2,0,1:T(8,128)S(1)}, u32[]{:S(2)}, u32[]{:S(2)}) %all-to-all-start.3) | async-done | bytes 1769504 | tf_op jit(solution)/shard_map/all_to_all | solution.py:34
  504.1 8.6 reshape.821
  512.7 5.7 copy.158
  518.4 5.1 fusion.34
  523.6 0.8 slice_multiply_fusion.4
  525.6 15.9 %fusion.22 = f32[24,8,2,24,2,48]{5,3,0,2,1,4:T(8,128)S(1)} fusion(f32[1,192,24,2,48]{1,4,2,3,0:T(8,128)S(1)} %maximum_bitcast_fusion.5, f32[1,192,24,2,48]{1,4,2,3,0:T(8,128)S(1)} %maximum_bitcast_fusion.4, f32[1,192,1,8,24]{1,4,0,3,2:T(8,128)S(1)} %copy-done.4, f32[1,192,1,8,24]{1,4,0,3,2:T(8,128)S(1)} %copy-done.3, ...), kind=kOutput, calls=%fused_computation.27 | convolution fusion | flops 4078190592 | bytes 7520256 | tf_op jit(solution)/shard_map/fkyrx,rksdz->ydfzsx/dot_general | solution.py:105
  541.5 8.0 copy.196
  549.5 16.6 %reshape.868 = f32[24,8,4608]{2,0,1:T(8,128)} reshape(f32[24,8,2,24,2,48]{5,4,3,2,0,1:T(2,128)} %copy.196) | data formatting | bytes 7077888 | tf_op jit(solution)/shard_map/reshape | solution.py:106
  566.1 4.5 all-to-all-start.4
  570.6 0.9 fusion.107
  571.5 77.6 %all-to-all-done.4 = f32[24,8,4608]{2,0,1:T(8,128)} async-done(((f32[24,8,4608]{2,0,1:T(8,128)}), f32[24,8,4608]{2,0,1:T(8,128)}, u32[]{:S(2)}, u32[]{:S(2)}) %all-to-all-start.4) | async-done | bytes 3538976 | tf_op jit(solution)/shard_map/all_to_all | solution.py:34
  649.2 17.3 %reshape.823 = f32[192,2,24,2,48]{4,3,2,1,0:T(2,128)} reshape(f32[8,24,1,4608]{3,1,0,2:T(8,128)} %bitcast.63) | data formatting | bytes 7077888 | tf_op jit(solution)/shard_map/reshape | solution.py:107
  666.5 24.9 %fusion.19 = f32[48,4,2,24,2,48]{0,5,3,2,1,4:T(8,128)} fusion(f32[192,2,24,2,48,1,1]{4,3,2,1,0,6,5:T(2,128)} %bitcast.221, f32[1,192,1,4,48]{1,4,0,3,2:T(8,128)S(1)} %get-tuple-element.20, f32[1,192,1,4,48]{1,4,0,3,2:T(8,128)S(1)} %get-tuple-element.19, f32[1,192,1,4,48]{1,4,0,3,2:T(8,128)S(1)} %get-tuple-element.18), kind=kOutput, calls=%fused_computation.26 | convolution fusion | flops 4077305856 | bytes 7520256 | tf_op jit(solution)/shard_map/kfzrx,rksby->xbfzsy/dot_general | solution.py:109
  691.4 13.7 %copy.163 = f32[48,4,2,24,2,48]{5,4,3,2,0,1:T(2,128)} copy(f32[48,4,2,24,2,48]{0,5,3,2,1,4:T(8,128)} %fusion.19) | data formatting | bytes 7077888 | tf_op jit(solution)/shard_map/kfzrx,rksby->xbfzsy/transpose | solution.py:109
  705.1 16.6 %reshape.824 = f32[48,4,4608]{2,0,1:T(8,128)} reshape(f32[48,4,2,24,2,48]{5,4,3,2,0,1:T(2,128)} %copy.163) | data formatting | bytes 7077888 | tf_op jit(solution)/shard_map/reshape | solution.py:110
  721.7 46.9 %all_to_all.84 = f32[48,4,4608]{2,0,1:T(8,128)} all-to-all(f32[48,4,4608]{2,0,1:T(8,128)} %reshape.824), channel_id=1, replica_groups=mesh['band'=4,'px'=4,'py'=2] {'px'}, dimensions={1} | all-to-all | bytes 7077888 | tf_op jit(solution)/shard_map/all_to_all | solution.py:30
  768.6 17.1 %reshape.825 = f32[192,2,24,2,48]{4,3,2,1,0:T(2,128)} reshape(f32[4,48,1,4608]{3,1,0,2:T(8,128)} %bitcast.230) | data formatting | bytes 7077888 | tf_op jit(solution)/shard_map/reshape | solution.py:111
  785.7 13.2 %copy.164 = f32[192,2,24,2,48]{0,4,3,2,1:T(8,128)} copy(f32[192,2,24,2,48]{4,3,2,1,0:T(2,128)} %reshape.825) | data formatting | bytes 7077888 | tf_op jit(solution)/shard_map/reshape | solution.py:111
  798.9 10.6 fusion.9
  810.1 1.0 copy-done.2
  811.1 3.1 fusion.41
  814.3 2.6 pad_maximum_fusion
  816.9 320.8 %all-gather.3.cloned.1.call-done = f32[16,24,48,192]{3,2,1,0:T(8,128)} async-done(((f32[4,24,48,192]{3,2,1,0:T(8,128)}), f32[16,24,48,192]{3,2,1,0:T(8,128)}) %all-gather.3.cloned.1.call-update) | async-done | bytes 14155792 | tf_op jit(solution)/shard_map/all_gather | solution.py:120
  1137.7 4.9 slice.59
  1142.6 11.4 slice.60
  1154.1 11.8 %copy.166 = f32[3,4,24,48,192]{4,3,2,1,0:T(8,128)} copy(f32[3,4,24,48,192]{4,3,2,0,1:T(8,128)} %slice.60) | data formatting | bytes 21233664 | tf_op jit(solution)/shard_map/slice | solution.py:169
  (43 shorter events, 6.9 us)
Async XLA Ops:
  7.2 2.2 copy-start
  8.1 10.4 copy-start.5
  12.6 8.6 all-to-all-start
  192.9 45.9 %all-to-all-start.1 = ((bf16[4,2,221184]{2,1,0:T(2,128)(2,1)}), bf16[4,2,221184]{2,1,0:T(2,128)(2,1)}, u32[]{:S(2)}, u32[]{:S(2)}) async-start(bf16[4,2,221184]{2,1,0:T(2,128)(2,1)} %reshape.873), calls=%async_computation.1 | async-start | bytes 7077888 | tf_op jit(solution)/shard_map/all_to_all | solution.py:156
  197.6 176.5 %reduce-scatter.2.cloned.1.call-start = ((), (), s32[]{:S(2)}) async-start(), calls=%async_computation.7 | async-start | bytes 5898240 | tf_op jit(solution)/shard_map/reduce_scatter | solution.py:164
  397.7 25.9 %all-to-all-start.2 = ((f32[48,4,2304]{2,0,1:T(8,128)}), f32[48,4,2304]{2,0,1:T(8,128)S(1)}, u32[]{:S(2)}, u32[]{:S(2)}) async-start(f32[48,4,2304]{2,0,1:T(8,128)} %reshape.818), calls=%async_computation.3 | async-start | bytes 3538944 | tf_op jit(solution)/shard_map/all_to_all | solution.py:30
  458.1 46.0 %all-to-all-start.3 = ((f32[24,8,2304]{2,0,1:T(8,128)}), f32[24,8,2304]{2,0,1:T(8,128)S(1)}, u32[]{:S(2)}, u32[]{:S(2)}) async-start(f32[24,8,2304]{2,0,1:T(8,128)} %reshape.867), calls=%async_computation.4 | async-start | bytes 3538944 | tf_op jit(solution)/shard_map/all_to_all | solution.py:34
  524.6 0.9 copy-start.3
  524.6 1.0 copy-start.4
  566.1 83.1 %all-to-all-start.4 = ((f32[24,8,4608]{2,0,1:T(8,128)}), f32[24,8,4608]{2,0,1:T(8,128)}, u32[]{:S(2)}, u32[]{:S(2)}) async-start(f32[24,8,4608]{2,0,1:T(8,128)} %reshape.868), calls=%async_computation.5 | async-start | bytes 7077888 | tf_op jit(solution)/shard_map/all_to_all | solution.py:34
  570.6 567.1 %all-gather.3.cloned.1.call-start = ((), (), s32[]{:S(2)}) async-start(), calls=%async_computation.8 | async-start | bytes 23592960 | tf_op jit(solution)/shard_map/all_gather | solution.py:120
  809.9 1.3 copy-start.2
  1154.1 11.8 %copy-start.1 = (bf16[1,128,384]{2,1,0:T(8,128)(2,1)S(1)}, bf16[1,128,384]{2,1,0:T(8,128)(2,1)}, u32[]{:S(2)}) copy-start(bf16[1,128,384]{2,1,0:T(8,128)(2,1)} %param.4) | copy-start | bytes 294916
Sparse Core Ops, SparseCore 0:
  288.9 85.1 reduce-scatter.1
  817.0 320.6 all-gather.2
